TPU v7x, 32 devices: a whole 2x2x4 slice. The times are simulated.
32 devices in a mesh: task: 4 (over y, x), param: 8 (over z, core).
Axes of the slice: x: 2, y: 2, z: 4, core: 2. Of those that a mesh axis runs over, the one named last changes fastest.
Arguments:
- grads: bfloat16 [8, 2048, 4096], P('task', 'param')
- order: int32 [8], replicated, may hold values from 0 to 7, each once
Outputs:
- update: float32 [2048, 4096], P('param', 'task')
All inputs are finite; a program needn't handle non-finite values.
Results may differ from a plain program's by a relative error of at most 0.0003.
Values may be sent and summed in bfloat16 or wider, within the bound.
A program may use at most 64 MiB of HBM per device.

v0:
```python
import functools

import jax
import jax.numpy as jnp
from jax import lax
from jax.experimental import pallas as pl
from jax.experimental.pallas import tpu as pltpu
from jax.sharding import PartitionSpec as P

MESH = pl.DeviceIdType.MESH
LANES = 128
TILE = 16
CHUNKS = 8
OUT_CHUNKS = 4


def kernel(
    n_task, n_param, entries,
    order_hbm, grads_ref, out_ref,
    order_ref, mine, held, gp, gt,
    order_sem, own_sem, send_sem, recv_sem, p_send, p_recv, t_send, t_recv, out_sem,
):
    tasks_here, rows, _ = grads_ref.shape
    total, _, block = mine.shape
    lane_blocks = block // LANES
    chunk = rows // CHUNKS
    t = lax.axis_index("task")
    p = lax.axis_index("param")

    def to_t(d):
        if n_task == 4:
            return (t + 1 - 2 * lax.rem(t, 2), lax.rem(t + 2, 4), 3 - t)[d - 1]
        return lax.rem(t + d, n_task)

    def from_t(d):
        return to_t(d) if n_task == 4 else lax.rem(t - d + n_task, n_task)

    def peer_t(d):
        return {"task": to_t(d)}

    def peer_p(d):
        return {"param": lax.rem(p + d, n_param)}

    def cols(of):
        return pl.ds(pl.multiple_of(of * block, LANES), block)

    def rows_of(c):
        return pl.ds(pl.multiple_of(c * chunk, TILE), chunk)

    def exchange(d, c, slot):
        return pltpu.make_async_remote_copy(
            src_ref=grads_ref.at[:, rows_of(c), cols(to_t(d))],
            dst_ref=mine.at[pl.ds(slot * tasks_here, tasks_here), rows_of(c), :],
            send_sem=send_sem.at[d - 1, c],
            recv_sem=recv_sem.at[d - 1, c],
            device_id=peer_t(d),
            device_id_type=MESH,
        )

    def local(c):
        return pltpu.make_async_copy(
            grads_ref.at[:, rows_of(c), cols(t)],
            mine.at[pl.ds(t * tasks_here, tasks_here), rows_of(c), :],
            own_sem.at[c],
        )

    barrier = pltpu.get_barrier_semaphore()
    for d in range(1, n_task):
        pl.semaphore_signal(barrier, inc=1, device_id=peer_t(d), device_id_type=MESH)
    for d in range(1, n_param):
        pl.semaphore_signal(barrier, inc=1, device_id=peer_p(d), device_id_type=MESH)
    pl.semaphore_wait(barrier, n_task + n_param - 2)

    far = n_task - 1
    for c in range(CHUNKS):
        exchange(far, c, t).start()
    for c in range(CHUNKS):
        local(c).start()
    get_order = pltpu.make_async_copy(order_hbm, order_ref, order_sem)
    get_order.start()
    for c in range(CHUNKS):
        for d in range(1, far):
            exchange(d, c, t).start()

    pairs = [(i, j) for i in range(total) for j in range(i, total)]
    steps = chunk // TILE * lane_blocks

    def tile_of(q):
        r = pl.multiple_of(q // lane_blocks * TILE, TILE)
        l = pl.multiple_of(q % lane_blocks * LANES, LANES)
        return pl.ds(r, TILE), pl.ds(l, LANES)

    def gram_chunk(c, accs):
        local(c).wait()
        for d in range(1, n_task):
            exchange(d, c, from_t(d)).wait_recv()

        def step(q, accs):
            r, l = tile_of(q + c * steps)
            x = [mine[m, r, l].astype(jnp.float32) for m in range(total)]
            out = []
            for acc, (i, j) in zip(accs, pairs):
                prod = x[i] * x[j]
                out.append(acc + (prod[:8] + prod[8:]))
            return tuple(out)

        return lax.fori_loop(0, steps, step, accs)

    zero = jnp.zeros((8, LANES), jnp.float32)
    accs = lax.fori_loop(0, CHUNKS, gram_chunk, (zero,) * len(pairs))

    sub = lax.broadcasted_iota(jnp.int32, (8, LANES), 0)
    lane = lax.broadcasted_iota(jnp.int32, (8, LANES), 1)
    by_pair = dict(zip(pairs, accs))
    summed = {
        k: jnp.broadcast_to(jnp.sum(v, axis=0, keepdims=True), (8, LANES))
        for k, v in by_pair.items()
    }
    packed = zero
    for i in range(total):
        stacked = zero
        for j in range(total):
            stacked = jnp.where(sub == j, summed[min(i, j), max(i, j)], stacked)
        here = lane == sub * total + i
        packed = jnp.where(here, jnp.sum(stacked, axis=1, keepdims=True), packed)

    gp[p] = jnp.sum(packed, axis=0, keepdims=True)

    def send_p(d, slot):
        return pltpu.make_async_remote_copy(
            src_ref=gp.at[p], dst_ref=gp.at[slot],
            send_sem=p_send.at[d - 1], recv_sem=p_recv.at[d - 1],
            device_id=peer_p(d), device_id_type=MESH,
        )

    def send_t(d, slot):
        return pltpu.make_async_remote_copy(
            src_ref=gt.at[t], dst_ref=gt.at[slot],
            send_sem=t_send.at[d - 1], recv_sem=t_recv.at[d - 1],
            device_id=peer_t(d), device_id_type=MESH,
        )

    for d in range(1, n_param):
        send_p(d, p).start()
    for d in range(1, n_param):
        send_p(d, lax.rem(p - d + n_param, n_param)).wait_recv()
    part = gp[0]
    for k in range(1, n_param):
        part = part + gp[k]
    gt[t] = part
    for d in range(1, n_task):
        send_t(d, t).start()
    for d in range(1, n_task):
        send_t(d, from_t(d)).wait_recv()
    gram = gt[0]
    for k in range(1, n_task):
        gram = gram + gt[k]
    gram = jnp.broadcast_to(gram, (8, LANES))

    get_order.wait()
    coefs = jnp.where((sub == lane) & (sub < total), 1.0, 0.0)
    columns, norms = [], []
    for k in range(total):
        j = order_ref[k]
        column = jnp.sum(jnp.where(lane == sub * total + j, gram, 0.0), axis=1, keepdims=True)
        column = jnp.broadcast_to(column, (8, LANES))
        columns.append(column)
        norms.append(jnp.sum(jnp.where(sub == j, column, 0.0), axis=0, keepdims=True))
    for k in range(total):
        j = order_ref[k]
        d = jnp.sum(coefs * columns[k], axis=0, keepdims=True)
        w = jnp.minimum(d, 0.0) / (norms[k] + 1e-06)
        w = jnp.broadcast_to(w, (8, LANES))
        coefs = coefs - jnp.where((sub == j) & (lane != j), w, 0.0)
    weight = jnp.broadcast_to(jnp.sum(coefs, axis=1, keepdims=True), (8, LANES))
    spread = jnp.where(lax.rem(lane, total) == sub, weight, 0.0)
    across = jnp.sum(spread, axis=0, keepdims=True)
    row_m = (lane >= sub * total) & (lane < sub * total + total)
    half = jnp.sum(jnp.where(row_m, gram * across, 0.0), axis=1, keepdims=True)
    energy = jnp.sum(weight * half, axis=0, keepdims=True)
    rms = jnp.sqrt(jnp.maximum(energy, 0.0) / entries + 1e-06)
    scaled = weight * (0.5 / rms)
    each = [jnp.broadcast_to(scaled[m : m + 1, :], (TILE, LANES)) for m in range(total)]

    out_rows = rows // OUT_CHUNKS
    out_steps = out_rows // TILE * lane_blocks

    def put(c):
        r = pl.ds(c * out_rows, out_rows)
        return pltpu.make_async_copy(held.at[r, :], out_ref.at[r, :], out_sem.at[c])

    def combine(q, carry):
        r, l = tile_of(q)
        v = each[0] * mine[0, r, l].astype(jnp.float32)
        for m in range(1, total):
            v = v + each[m] * mine[m, r, l].astype(jnp.float32)
        held[r, l] = v
        return carry

    for c in range(OUT_CHUNKS):
        lax.fori_loop(c * out_steps, (c + 1) * out_steps, combine, 0, unroll=4)
        put(c).start()
    for c in range(OUT_CHUNKS):
        put(c).wait()
    for c in range(CHUNKS):
        for d in range(1, n_task):
            exchange(d, c, t).wait_send()
    for d in range(1, n_param):
        send_p(d, p).wait_send()
    for d in range(1, n_task):
        send_t(d, t).wait_send()


def shards(mesh, grads, order):
    n_task, n_param = mesh.shape["task"], mesh.shape["param"]
    tasks_here, rows, width = grads.shape
    total, block = tasks_here * n_task, width // n_task
    entries = float(rows * n_param * width)
    dma = pltpu.SemaphoreType.DMA
    return pl.pallas_call(
        functools.partial(kernel, n_task, n_param, entries),
        out_shape=jax.ShapeDtypeStruct((rows, block), jnp.float32),
        in_specs=[
            pl.BlockSpec(memory_space=pltpu.HBM),
            pl.BlockSpec(memory_space=pltpu.HBM),
        ],
        out_specs=pl.BlockSpec(memory_space=pl.ANY),
        scratch_shapes=[
            pltpu.SMEM((total,), jnp.int32),
            pltpu.VMEM((total, rows, block), jnp.bfloat16),
            pltpu.VMEM((rows, block), jnp.float32),
            pltpu.VMEM((n_param, 1, LANES), jnp.float32),
            pltpu.VMEM((n_task, 1, LANES), jnp.float32),
            dma(()),
            dma((CHUNKS,)),
            dma((n_task - 1, CHUNKS)),
            dma((n_task - 1, CHUNKS)),
            dma((n_param - 1,)),
            dma((n_param - 1,)),
            dma((n_task - 1,)),
            dma((n_task - 1,)),
            dma((OUT_CHUNKS,)),
        ],
        compiler_params=pltpu.CompilerParams(collective_id=0, has_side_effects=True),
    )(order, grads)


def solution(mesh):
    placed = (P("task", "param", None), P())
    return jax.shard_map(
        functools.partial(shards, mesh),
        mesh=mesh, in_specs=placed, out_specs=P("param", "task"), check_vma=False,
    )
```

profile of v0, /device:TPU:0, one launch (start us, length us, event | category | flops | bytes accessed | tf_op | source)
XLA Modules:
  0.0 64.8 jit_solution(15571165710490158120)
XLA Ops:
  0.0 62.5 %shard_map.28 = f32[256,1024]{1,0:T(8,128)} custom-call(s32[8]{0:T(128)} %order_hbm.1, bf16[2,256,4096]{2,1,0:T(8,128)(2,1)} %grads_ref.1), custom_call_target="tpu_custom_call" | custom-call | tf_op jit(solution)/shard_map/pallas_call | solution.py:220
  62.5 2.3 %copy.4 = f32[256,1024]{1,0:T(8,128)} copy(f32[256,1024]{1,0:T(8,128)} %shard_map.28) | data formatting | bytes 2097152
where the time goes:
time: 64.9 us; the launch traced here: 64.8 us
  Pallas kernels  62.5 us (96%)
  local copies, waits for them, and re-layouts  2.31 us (4%)
    pallas_call x1, Pallas kernels, shards(): pl.pallas_call(functools.partial(kernel, n_task, n_param, entries), out_s...  62.5 us
    unnamed x1, local copies, waits for them, and re-layouts  2.31 us

commit v1 on v0

--- a/solution.py
+++ b/solution.py
@@ -11,14 +11,13 @@
 LANES = 128
 TILE = 16
 CHUNKS = 8
-OUT_CHUNKS = 4
 
 
 def kernel(
     n_task, n_param, entries,
     order_hbm, grads_ref, out_ref,
-    order_ref, mine, held, gp, gt,
-    order_sem, own_sem, send_sem, recv_sem, p_send, p_recv, t_send, t_recv, out_sem,
+    order_ref, mine, gp, gt,
+    order_sem, own_sem, send_sem, recv_sem, p_send, p_recv, t_send, t_recv,
 ):
     tasks_here, rows, _ = grads_ref.shape
     total, _, block = mine.shape
@@ -182,26 +181,15 @@
     scaled = weight * (0.5 / rms)
     each = [jnp.broadcast_to(scaled[m : m + 1, :], (TILE, LANES)) for m in range(total)]
 
-    out_rows = rows // OUT_CHUNKS
-    out_steps = out_rows // TILE * lane_blocks
-
-    def put(c):
-        r = pl.ds(c * out_rows, out_rows)
-        return pltpu.make_async_copy(held.at[r, :], out_ref.at[r, :], out_sem.at[c])
-
     def combine(q, carry):
         r, l = tile_of(q)
         v = each[0] * mine[0, r, l].astype(jnp.float32)
         for m in range(1, total):
             v = v + each[m] * mine[m, r, l].astype(jnp.float32)
-        held[r, l] = v
+        out_ref[r, l] = v
         return carry
 
-    for c in range(OUT_CHUNKS):
-        lax.fori_loop(c * out_steps, (c + 1) * out_steps, combine, 0, unroll=4)
-        put(c).start()
-    for c in range(OUT_CHUNKS):
-        put(c).wait()
+    lax.fori_loop(0, rows // TILE * lane_blocks, combine, 0, unroll=4)
     for c in range(CHUNKS):
         for d in range(1, n_task):
             exchange(d, c, t).wait_send()
@@ -219,16 +207,15 @@
     dma = pltpu.SemaphoreType.DMA
     return pl.pallas_call(
         functools.partial(kernel, n_task, n_param, entries),
-        out_shape=jax.ShapeDtypeStruct((rows, block), jnp.float32),
+        out_shape=pltpu.VMEM((rows, block), jnp.float32),
         in_specs=[
             pl.BlockSpec(memory_space=pltpu.HBM),
             pl.BlockSpec(memory_space=pltpu.HBM),
         ],
-        out_specs=pl.BlockSpec(memory_space=pl.ANY),
+        out_specs=pl.BlockSpec(memory_space=pltpu.VMEM),
         scratch_shapes=[
             pltpu.SMEM((total,), jnp.int32),
             pltpu.VMEM((total, rows, block), jnp.bfloat16),
-            pltpu.VMEM((rows, block), jnp.float32),
             pltpu.VMEM((n_param, 1, LANES), jnp.float32),
             pltpu.VMEM((n_task, 1, LANES), jnp.float32),
             dma(()),
@@ -239,7 +226,6 @@
             dma((n_param - 1,)),
             dma((n_task - 1,)),
             dma((n_task - 1,)),
-            dma((OUT_CHUNKS,)),
         ],
         compiler_params=pltpu.CompilerParams(collective_id=0, has_side_effects=True),
     )(order, grads)

time: 64.9 us -> 62.8 us (0.968)
  local copies, waits for them, and re-layouts: 2.31 us -> 0.97 us
  Pallas kernels: 62.5 us -> 61.7 us
    unnamed x1, local copies, waits for them, and re-layouts: 2.31 us -> 0.97 us
    pallas_call x1, Pallas kernels: 62.5 us -> 61.7 us  [shards(): pl.pallas_call(functools.partial(kernel, n_task, n_param, entries), out_s...]
where the time goes in v1:
time: 62.8 us; the launch traced here: 62.7 us
  Pallas kernels  61.7 us (98%)
  local copies, waits for them, and re-layouts  0.97 us (2%)
    pallas_call x1, Pallas kernels, shards(): pl.pallas_call(functools.partial(kernel, n_task, n_param, entries), out_s...  61.7 us

profile of v1, /device:TPU:0, one launch (start us, length us, event | category | flops | bytes accessed | tf_op | source)
XLA Modules:
  0.0 62.7 jit_solution(7935900821822930770)
XLA Ops:
  0.0 61.7 %shard_map.28 = f32[256,1024]{1,0:T(8,128)S(1)} custom-call(s32[8]{0:T(128)} %order_hbm.1, bf16[2,256,4096]{2,1,0:T(8,128)(2,1)} %grads_ref.1), custom_call_target="tpu_custom_call" | custom-call | tf_op jit(solution)/shard_map/pallas_call | solution.py:208
  61.7 1.0 %copy.4 = f32[256,1024]{1,0:T(8,128)} copy(f32[256,1024]{1,0:T(8,128)S(1)} %shard_map.28) | data formatting | bytes 2097152

commit v2 on v1

--- a/solution.py
+++ b/solution.py
@@ -16,8 +16,8 @@
 def kernel(
     n_task, n_param, entries,
     order_hbm, grads_ref, out_ref,
-    order_ref, mine, gp, gt,
-    order_sem, own_sem, send_sem, recv_sem, p_send, p_recv, t_send, t_recv,
+    order_ref, mine, parts,
+    order_sem, own_sem, send_sem, recv_sem, g_send, g_recv, known,
 ):
     tasks_here, rows, _ = grads_ref.shape
     total, _, block = mine.shape
@@ -37,8 +37,27 @@
     def peer_t(d):
         return {"task": to_t(d)}
 
-    def peer_p(d):
-        return {"param": lax.rem(p + d, n_param)}
+    pair = 2 if n_param % 2 == 0 else 1
+    close = (1, 2) if n_task == 4 else tuple(range(1, n_task))
+    up, down = p + pair < n_param, p >= pair
+    degree = len(close) + pair - 1 + up.astype(jnp.int32) + down.astype(jnp.int32)
+
+    def greet(sem):
+        for d in close:
+            pl.semaphore_signal(sem, inc=1, device_id=peer_t(d), device_id_type=MESH)
+        if pair == 2:
+            other = {"param": p + 1 - 2 * lax.rem(p, 2)}
+            pl.semaphore_signal(sem, inc=1, device_id=other, device_id_type=MESH)
+
+        @pl.when(up)
+        def _():
+            pl.semaphore_signal(sem, inc=1, device_id={"param": p + pair}, device_id_type=MESH)
+
+        @pl.when(down)
+        def _():
+            pl.semaphore_signal(sem, inc=1, device_id={"param": p - pair}, device_id_type=MESH)
+
+        pl.semaphore_wait(sem, degree)
 
     def cols(of):
         return pl.ds(pl.multiple_of(of * block, LANES), block)
@@ -63,23 +82,26 @@
             own_sem.at[c],
         )
 
-    barrier = pltpu.get_barrier_semaphore()
+    greet(pltpu.get_barrier_semaphore())
+    rounds = spread_rounds(n_task, n_param)
+    for d in close:
+        exchange(d, 0, t).start()
+    for k in range(min(1, rounds)):
+        greet(known.at[k])
     for d in range(1, n_task):
-        pl.semaphore_signal(barrier, inc=1, device_id=peer_t(d), device_id_type=MESH)
-    for d in range(1, n_param):
-        pl.semaphore_signal(barrier, inc=1, device_id=peer_p(d), device_id_type=MESH)
-    pl.semaphore_wait(barrier, n_task + n_param - 2)
-
-    far = n_task - 1
-    for c in range(CHUNKS):
-        exchange(far, c, t).start()
+        if d not in close:
+            for c in range(CHUNKS):
+                exchange(d, c, t).start()
+    for c in range(1, CHUNKS):
+        for d in close:
+            exchange(d, c, t).start()
     for c in range(CHUNKS):
         local(c).start()
     get_order = pltpu.make_async_copy(order_hbm, order_ref, order_sem)
     get_order.start()
-    for c in range(CHUNKS):
-        for d in range(1, far):
-            exchange(d, c, t).start()
+    for k in range(1, rounds):
+        greet(known.at[k])
+    get_order.wait()
 
     pairs = [(i, j) for i in range(total) for j in range(i, total)]
     steps = chunk // TILE * lane_blocks
@@ -123,40 +145,36 @@
         here = lane == sub * total + i
         packed = jnp.where(here, jnp.sum(stacked, axis=1, keepdims=True), packed)
 
-    gp[p] = jnp.sum(packed, axis=0, keepdims=True)
-
-    def send_p(d, slot):
+    me = p * n_task + t
+    everyone = [(dp, dt) for dp in range(n_param) for dt in range(n_task) if dp or dt]
+    everyone.sort(key=lambda k: abs(k[0] - n_param // 2))
+    parts[me] = jnp.sum(packed, axis=0, keepdims=True)
+
+    def share(k):
+        dp, dt = everyone[k]
         return pltpu.make_async_remote_copy(
-            src_ref=gp.at[p], dst_ref=gp.at[slot],
-            send_sem=p_send.at[d - 1], recv_sem=p_recv.at[d - 1],
-            device_id=peer_p(d), device_id_type=MESH,
+            src_ref=parts.at[me], dst_ref=parts.at[me],
+            send_sem=g_send, recv_sem=g_recv,
+            device_id={"param": lax.rem(p + dp, n_param), "task": lax.rem(t + dt, n_task)},
+            device_id_type=MESH,
         )
 
-    def send_t(d, slot):
-        return pltpu.make_async_remote_copy(
-            src_ref=gt.at[t], dst_ref=gt.at[slot],
-            send_sem=t_send.at[d - 1], recv_sem=t_recv.at[d - 1],
-            device_id=peer_t(d), device_id_type=MESH,
-        )
-
-    for d in range(1, n_param):
-        send_p(d, p).start()
-    for d in range(1, n_param):
-        send_p(d, lax.rem(p - d + n_param, n_param)).wait_recv()
-    part = gp[0]
-    for k in range(1, n_param):
-        part = part + gp[k]
-    gt[t] = part
-    for d in range(1, n_task):
-        send_t(d, t).start()
-    for d in range(1, n_task):
-        send_t(d, from_t(d)).wait_recv()
-    gram = gt[0]
-    for k in range(1, n_task):
-        gram = gram + gt[k]
-    gram = jnp.broadcast_to(gram, (8, LANES))
-
-    get_order.wait()
+    def shared(sem):
+        count = pl.ds(0, len(everyone))
+        return pltpu.make_async_copy(parts.at[count], parts.at[count], sem)
+
+    for k in range(len(everyone)):
+        share(k).start()
+    for c in range(CHUNKS):
+        for d in range(1, n_task):
+            exchange(d, c, t).wait_send()
+    shared(g_recv).wait()
+    terms = [parts[k] for k in range(n_task * n_param)]
+    while len(terms) > 1:
+        odd = terms[len(terms) - len(terms) % 2 :]
+        terms = [a + b for a, b in zip(terms[0::2], terms[1::2])] + odd
+    gram = jnp.broadcast_to(terms[0], (8, LANES))
+
     coefs = jnp.where((sub == lane) & (sub < total), 1.0, 0.0)
     columns, norms = [], []
     for k in range(total):
@@ -190,13 +208,12 @@
         return carry
 
     lax.fori_loop(0, rows // TILE * lane_blocks, combine, 0, unroll=4)
-    for c in range(CHUNKS):
-        for d in range(1, n_task):
-            exchange(d, c, t).wait_send()
-    for d in range(1, n_param):
-        send_p(d, p).wait_send()
-    for d in range(1, n_task):
-        send_t(d, t).wait_send()
+    shared(g_send).wait()
+
+
+def spread_rounds(n_task, n_param):
+    pair = 2 if n_param % 2 == 0 else 1
+    return (2 if n_task == 4 else 1) + pair - 1 + n_param // pair - 1 - 1
 
 
 def shards(mesh, grads, order):
@@ -216,16 +233,14 @@
         scratch_shapes=[
             pltpu.SMEM((total,), jnp.int32),
             pltpu.VMEM((total, rows, block), jnp.bfloat16),
-            pltpu.VMEM((n_param, 1, LANES), jnp.float32),
-            pltpu.VMEM((n_task, 1, LANES), jnp.float32),
+            pltpu.VMEM((n_task * n_param, 1, LANES), jnp.float32),
             dma(()),
             dma((CHUNKS,)),
             dma((n_task - 1, CHUNKS)),
             dma((n_task - 1, CHUNKS)),
-            dma((n_param - 1,)),
-            dma((n_param - 1,)),
-            dma((n_task - 1,)),
-            dma((n_task - 1,)),
+            dma(()),
+            dma(()),
+            pltpu.SemaphoreType.REGULAR((max(1, spread_rounds(n_task, n_param)),)),
         ],
         compiler_params=pltpu.CompilerParams(collective_id=0, has_side_effects=True),
     )(order, grads)

time: 62.8 us -> 60.6 us (0.965)
  Pallas kernels: 61.7 us -> 59.5 us
    pallas_call x1, Pallas kernels: 61.7 us -> 59.5 us  [shards(): pl.pallas_call(functools.partial(kernel, n_task, n_param, entries), out_s...]
where the time goes in v2:
time: 60.6 us; the launch traced here: 60.4 us
  Pallas kernels  59.5 us (98%)
  local copies, waits for them, and re-layouts  0.97 us (2%)
    pallas_call x1, Pallas kernels, shards(): pl.pallas_call(functools.partial(kernel, n_task, n_param, entries), out_s...  59.5 us

profile of v2, /device:TPU:0, one launch (start us, length us, event | category | flops | bytes accessed | tf_op | source)
XLA Modules:
  0.0 60.4 jit_solution(12805799456563166308)
XLA Ops:
  0.0 59.5 %shard_map.28 = f32[256,1024]{1,0:T(8,128)S(1)} custom-call(s32[8]{0:T(128)} %order_hbm.1, bf16[2,256,4096]{2,1,0:T(8,128)(2,1)} %grads_ref.1), custom_call_target="tpu_custom_call" | custom-call | tf_op jit(solution)/shard_map/pallas_call | solution.py:225
  59.5 1.0 %copy.4 = f32[256,1024]{1,0:T(8,128)} copy(f32[256,1024]{1,0:T(8,128)S(1)} %shard_map.28) | data formatting | bytes 2097152
